TPU v7x, 256 devices: a whole 4x4x8 slice. The times are simulated.
256 devices in a mesh: grp: 4 (over x), chan: 64 (over y, z, core).
Axes of the slice: x: 4, y: 4, z: 8, core: 2. Of those that a mesh axis runs over, the one named last changes fastest.
Arguments:
- visibility: float32 [1024, 262144], P('chan', 'grp'), may hold values from -6 to 6
- interference_mask: int32 [1024, 131072], P(None, ('grp', 'chan')), may hold values from 0 to 1
- valid_time_count: int32 [4096], P(('grp', 'chan')), may hold values from 8 to 32
- fit_modes: float32 [1024, 32], P('grp'), may hold values from -1 to 1
Outputs:
- residual_vis: float32 [1024, 262144], P('chan', 'grp')
All inputs are finite; a program needn't handle non-finite values.
Results may differ from a plain program's by a relative error of at most 0.0003.
Values sent between devices are 32-bit elements; how exact they have to be, the bound alone decides.
A program may use at most 128 MiB of HBM per device.

v0:
```python
import jax
import jax.numpy as jnp
from jax import lax
from jax.sharding import PartitionSpec as P

damping = 0.1


def fit_weight(interference_mask, valid_time_count):
    antenna_pairs_list = valid_time_count.shape[0]
    sample_values = interference_mask.shape[1] // antenna_pairs_list
    projection_sums = lax.broadcasted_iota(jnp.int32, (antenna_pairs_list, sample_values), 1)
    within_range = (
        (projection_sums < valid_time_count[:, None])
        .astype(jnp.float32)
        .reshape(1, antenna_pairs_list * sample_values)
    )
    return (1.0 - interference_mask.astype(jnp.float32)) * within_range


def solve_normal(normal_matrix, target_signal):
    span_length = normal_matrix.shape[0]
    trailing = normal_matrix
    columns = []
    for position in range(span_length):
        column = trailing[:, 0] / jnp.sqrt(trailing[0, 0])
        columns.append(column)
        trailing = trailing[1:, 1:] - column[1:, None, :] * column[None, 1:, :]
    remains = target_signal
    forward = []
    for position in range(span_length):
        column = columns[position]
        current = remains[0] / column[0][None, :]
        forward.append(current)
        remains = remains[1:] - column[1:, None, :] * current[None]
    solution_values = [None] * span_length
    for position in reversed(range(span_length)):
        column = columns[position]
        current = forward[position]
        if position + 1 < span_length:
            later_rows = jnp.stack(solution_values[position + 1 :], 0)
            current = current - jnp.sum(column[1:, None, :] * later_rows, axis=0)
        solution_values[position] = current / column[0][None, :]
    return jnp.stack(solution_values, 0)


def solve_amplitudes(spectral_templates, assigned_rows, sample_weight, antenna_pairs_list):
    channel_count, span_length = spectral_templates.shape
    sample_values = sample_weight.shape[1] // antenna_pairs_list
    pairs = (spectral_templates[:, :, None] * spectral_templates[:, None, :]).reshape(
        channel_count, span_length * span_length
    )
    normal_matrix = lax.dot_general(
        pairs,
        sample_weight,
        (((0,), (0,)), ((), ())),
        precision=lax.Precision.HIGHEST,
        preferred_element_type=jnp.float32,
    )
    normal_matrix = normal_matrix.reshape(
        span_length, span_length, antenna_pairs_list * sample_values
    )
    normal_matrix = (
        normal_matrix + damping * jnp.eye(span_length, dtype=normal_matrix.dtype)[:, :, None]
    )
    weighted_values = assigned_rows.reshape(
        channel_count, antenna_pairs_list, 2, sample_values
    ) * sample_weight.reshape(channel_count, antenna_pairs_list, 1, sample_values)
    weighted_values = weighted_values.reshape(channel_count, antenna_pairs_list * 2 * sample_values)
    template_projection = lax.dot_general(
        spectral_templates,
        weighted_values,
        (((0,), (0,)), ((), ())),
        precision=lax.Precision.HIGHEST,
        preferred_element_type=jnp.float32,
    )
    target_signal = (
        template_projection.reshape(span_length, antenna_pairs_list, 2, sample_values)
        .transpose(0, 2, 1, 3)
        .reshape(span_length, 2, antenna_pairs_list * sample_values)
    )
    solution_values = solve_normal(normal_matrix, target_signal)
    return (
        solution_values.reshape(span_length, 2, antenna_pairs_list, sample_values)
        .transpose(0, 2, 1, 3)
        .reshape(span_length, antenna_pairs_list * 2 * sample_values)
    )


def per_device(visibility, interference_mask, valid_time_count, fit_modes):
    spectral_templates = lax.all_gather(fit_modes, "grp", axis=0, tiled=True)
    assigned_rows = lax.all_to_all(visibility, "chan", split_axis=1, concat_axis=0, tiled=True)
    antenna_pairs_list = valid_time_count.shape[0]
    sample_weight = fit_weight(interference_mask, valid_time_count)
    mode_amplitudes = solve_amplitudes(
        spectral_templates, assigned_rows, sample_weight, antenna_pairs_list
    )
    local_rows = visibility.shape[0]
    local_basis = lax.dynamic_slice_in_dim(
        spectral_templates, lax.axis_index("chan") * local_rows, local_rows, 0
    )
    model = jnp.dot(
        local_basis,
        lax.all_gather(mode_amplitudes, "chan", axis=1, tiled=True),
        precision=lax.Precision.HIGHEST,
        preferred_element_type=jnp.float32,
    )
    return visibility - model


def solution(mesh):
    placed = (P("chan", "grp"), P(None, ("grp", "chan")), P(("grp", "chan")), P("grp", None))
    return jax.shard_map(
        per_device, mesh=mesh, in_specs=placed, out_specs=P("chan", "grp"), check_vma=False
    )
```

profile of v0, /device:TPU:1, one launch (start us, length us, event | category | flops | bytes accessed | tf_op | source)
XLA Modules:
  0.0 266.8 jit_solution(13186309866033194750)
XLA Ops:
  6.5 4.7 %copy.120 = f32[2,64,8,1024]{3,2,0,1:T(8,128)} copy(f32[2,64,8,1024]{3,2,1,0:T(8,128)} %bitcast.366) | data formatting | bytes 8388608 | tf_op jit(solution)/shard_map/all_to_all | solution.py:92
  11.3 13.5 %all-to-all-start = ((f32[16,64,1024]{2,0,1:T(8,128)}), f32[16,64,1024]{2,0,1:T(8,128)}, u32[]{:S(2)}, u32[]{:S(2)}) async-start(f32[16,64,1024]{2,0,1:T(8,128)} %bitcast.367), calls=%async_computation | async-start | bytes 8388608 | tf_op jit(solution)/shard_map/all_to_all | solution.py:92
  25.0 10.6 %all_gather.6 = f32[1024,32]{0,1:T(8,128)S(1)} all-gather(f32[256,32]{0,1:T(8,128)S(1)} %copy-done.17), channel_id=1, replica_groups=mesh['grp'=4,'chan'=64] {'grp'}, dimensions={0}, use_global_device_ids=true | all-gather | bytes 163840 | tf_op jit(solution)/shard_map/all_gather | solution.py:91
  35.6 1.8 copy.48
  37.4 1.8 subtract_multiply_fusion
  39.3 6.7 %fusion.6 = f32[32,32,512]{2,1,0:T(8,128)S(1)} fusion(f32[1024,512]{0,1:T(8,128)S(1)} %subtract_multiply_fusion, f32[1024,32]{0,1:T(8,128)S(1)} %all_gather.6, f32[32,32]{1,0:T(8,128)S(1)} %fusion.13), kind=kOutput, calls=%fused_computation.17 | convolution fusion | flops 6444023808 | bytes 4329472 | tf_op jit(solution)/shard_map/dot_general | solution.py:53
  61.1 0.7 div.867
  61.8 2.5 mul.536
  64.3 5.3 %copy.49 = f32[1024,1024]{1,0:T(8,128)} copy(f32[1024,1024]{0,1:T(8,128)} %bitcast.368) | data formatting | bytes 8388608 | tf_op jit(solution)/shard_map/mul | solution.py:66
  69.7 50.9 %all-to-all-done = f32[16,64,1024]{2,0,1:T(8,128)} async-done(((f32[16,64,1024]{2,0,1:T(8,128)}), f32[16,64,1024]{2,0,1:T(8,128)}, u32[]{:S(2)}, u32[]{:S(2)}) %all-to-all-start) | async-done | bytes 4194336 | tf_op jit(solution)/shard_map/all_to_all | solution.py:92
  120.6 4.4 %bitcast_multiply_fusion = f32[1024,1024]{1,0:T(8,128)S(1)} fusion(f32[1024,1024]{1,0:T(8,128)} %copy.49, f32[16,64,1024]{2,0,1:T(8,128)} %all-to-all-done), kind=kLoop, calls=%fused_computation.4 | loop fusion | flops 1048576 | bytes 12582912 | tf_op jit(solution)/shard_map/mul | solution.py:66
  125.0 2.6 convolution_bitcast_fusion
  130.9 0.7 slice_subtract_fusion.58
  131.8 0.7 stack.184
  132.5 0.7 stack.183
  133.2 0.7 fusion.46
  133.9 0.7 stack.182
  134.6 0.7 fusion.45
  135.4 0.7 constant_dynamic-update-slice_fusion.4
  136.2 1.3 constant_dynamic-update-slice_fusion.10
  138.7 0.6 constant_dynamic-update-slice_fusion.7
  140.5 0.8 multiply_reduce_fusion.25
  141.2 1.3 constant_dynamic-update-slice_fusion.17
  142.5 0.7 stack.179
  143.8 0.6 constant_dynamic-update-slice_fusion.15
  144.4 0.6 constant_dynamic-update-slice_fusion.14
  146.8 0.8 multiply_reduce_fusion.24
  147.5 0.7 constant_dynamic-update-slice_fusion.25
  148.2 0.7 stack.178
  149.0 0.7 constant_dynamic-update-slice_fusion.34
  149.7 0.7 stack.177
  150.5 0.7 constant_dynamic-update-slice_fusion.44
  151.4 0.7 constant_dynamic-update-slice_fusion.55
  152.3 0.7 constant_dynamic-update-slice_fusion.67
  153.2 0.7 constant_dynamic-update-slice_fusion.80
  154.2 0.7 constant_dynamic-update-slice_fusion.94
  155.1 0.7 constant_dynamic-update-slice_fusion.109
  156.4 0.7 constant_dynamic-update-slice_fusion.142
  157.4 0.7 constant_dynamic-update-slice_fusion.160
  158.4 0.7 constant_dynamic-update-slice_fusion.179
  159.5 0.6 constant_dynamic-update-slice_fusion.199
  160.5 0.6 constant_dynamic-update-slice_fusion.220
  161.5 0.7 constant_dynamic-update-slice_fusion.242
  162.5 0.6 constant_dynamic-update-slice_fusion.265
  163.6 0.6 constant_dynamic-update-slice_fusion.289
  169.2 1.3 reshape.1023
  170.5 79.9 %all-gather.2.cloned.1.call-done = f32[32,65536]{1,0:T(8,128)} async-done(((f32[32,1024]{1,0:T(8,128)}), f32[32,65536]{1,0:T(8,128)}) %all-gather.2.cloned.1.call-update) | async-done | bytes 8388624 | tf_op jit(solution)/shard_map/all_gather | solution.py:104
  250.5 9.5 %convolution_subtract_fusion = f32[16,65536]{1,0:T(8,128)} fusion(f32[16,65536]{1,0:T(8,128)} %param.4, f32[32,65536]{1,0:T(8,128)} %all-gather.2.cloned.1.call-done, f32[1024,32]{0,1:T(8,128)S(1)} %all_gather.6, s32[]{:T(128)S(6)} %select_n.3), kind=kOutput, calls=%fused_computation | convolution fusion | flops 403701760 | bytes 16793604 | tf_op jit(solution)/shard_map/dot_general | solution.py:102
  (921 shorter events, 29.4 us)
Async XLA Ops:
  11.3 13.5 %copy-start.56 = (s32[16]{0:T(128)S(1)}, s32[16]{0:T(128)}, u32[]{:S(2)}) copy-start(s32[16]{0:T(128)} %param.6) | copy-start | bytes 196
  11.3 13.7 %copy-start.17 = (f32[256,32]{0,1:T(8,128)S(1)}, f32[256,32]{0,1:T(8,128)}, u32[]{:S(2)}) copy-start(f32[256,32]{0,1:T(8,128)} %param.7) | copy-start | bytes 98308
  11.3 24.4 %copy-start = (s32[1024,512]{1,0:T(8,128)S(1)}, s32[1024,512]{1,0:T(8,128)}, u32[]{:S(2)}) copy-start(s32[1024,512]{1,0:T(8,128)} %param.5) | copy-start | bytes 6291460
  11.3 109.3 %all-to-all-start = ((f32[16,64,1024]{2,0,1:T(8,128)}), f32[16,64,1024]{2,0,1:T(8,128)}, u32[]{:S(2)}, u32[]{:S(2)}) async-start(f32[16,64,1024]{2,0,1:T(8,128)} %bitcast.367), calls=%async_computation | async-start | bytes 8388608 | tf_op jit(solution)/shard_map/all_to_all | solution.py:92
  24.8 225.7 %all-gather.2.cloned.1.call-start = ((), (), s32[]{:S(2)}) async-start(), calls=%async_computation.1 | async-start | bytes 8519680 | tf_op jit(solution)/shard_map/all_gather | solution.py:104
  52.1 76.5 %copy-start.19 = (f32[1,512]{1,0:T(1,128)}, f32[1,512]{1,0:T(1,128)S(1)}, u32[]{:S(2)}) copy-start(f32[1,512]{1,0:T(1,128)S(1)} %slice.1010) | copy-start | bytes 6148
  52.1 76.6 %copy-start.21 = (f32[1,512]{1,0:T(1,128)}, f32[1,512]{1,0:T(1,128)S(1)}, u32[]{:S(2)}) copy-start(f32[1,512]{1,0:T(1,128)S(1)} %slice.1017) | copy-start | bytes 6148
  52.2 76.6 %copy-start.23 = (f32[1,512]{1,0:T(1,128)}, f32[1,512]{1,0:T(1,128)S(1)}, u32[]{:S(2)}) copy-start(f32[1,512]{1,0:T(1,128)S(1)} %slice.1024) | copy-start | bytes 6148
  52.2 76.7 %copy-start.25 = (f32[1,512]{1,0:T(1,128)}, f32[1,512]{1,0:T(1,128)S(1)}, u32[]{:S(2)}) copy-start(f32[1,512]{1,0:T(1,128)S(1)} %slice.1031) | copy-start | bytes 6148
  52.2 76.8 %copy-start.27 = (f32[1,512]{1,0:T(1,128)}, f32[1,512]{1,0:T(1,128)S(1)}, u32[]{:S(2)}) copy-start(f32[1,512]{1,0:T(1,128)S(1)} %slice.1038) | copy-start | bytes 6148
  52.2 77.0 %copy-start.29 = (f32[1,512]{1,0:T(1,128)}, f32[1,512]{1,0:T(1,128)S(1)}, u32[]{:S(2)}) copy-start(f32[1,512]{1,0:T(1,128)S(1)} %slice.1045) | copy-start | bytes 6148
  52.3 77.0 %copy-start.31 = (f32[1,512]{1,0:T(1,128)}, f32[1,512]{1,0:T(1,128)S(1)}, u32[]{:S(2)}) copy-start(f32[1,512]{1,0:T(1,128)S(1)} %slice.1052) | copy-start | bytes 6148
  52.3 77.1 %copy-start.33 = (f32[1,512]{1,0:T(1,128)}, f32[1,512]{1,0:T(1,128)S(1)}, u32[]{:S(2)}) copy-start(f32[1,512]{1,0:T(1,128)S(1)} %slice.1059) | copy-start | bytes 6148
  52.3 77.2 %copy-start.34 = (f32[1,512]{1,0:T(1,128)}, f32[1,512]{1,0:T(1,128)S(1)}, u32[]{:S(2)}) copy-start(f32[1,512]{1,0:T(1,128)S(1)} %slice.1066) | copy-start | bytes 6148
  52.3 77.2 %copy-start.35 = (f32[1,512]{1,0:T(1,128)}, f32[1,512]{1,0:T(1,128)S(1)}, u32[]{:S(2)}) copy-start(f32[1,512]{1,0:T(1,128)S(1)} %slice.1073) | copy-start | bytes 6148
  52.3 77.3 %copy-start.36 = (f32[1,512]{1,0:T(1,128)}, f32[1,512]{1,0:T(1,128)S(1)}, u32[]{:S(2)}) copy-start(f32[1,512]{1,0:T(1,128)S(1)} %slice.1080) | copy-start | bytes 6148
  52.4 77.4 %copy-start.37 = (f32[1,512]{1,0:T(1,128)}, f32[1,512]{1,0:T(1,128)S(1)}, u32[]{:S(2)}) copy-start(f32[1,512]{1,0:T(1,128)S(1)} %slice.1087) | copy-start | bytes 6148
  52.4 77.4 %copy-start.38 = (f32[1,512]{1,0:T(1,128)}, f32[1,512]{1,0:T(1,128)S(1)}, u32[]{:S(2)}) copy-start(f32[1,512]{1,0:T(1,128)S(1)} %slice.1094) | copy-start | bytes 6148
  52.4 77.5 %copy-start.39 = (f32[1,512]{1,0:T(1,128)}, f32[1,512]{1,0:T(1,128)S(1)}, u32[]{:S(2)}) copy-start(f32[1,512]{1,0:T(1,128)S(1)} %slice.1101) | copy-start | bytes 6148
  52.4 77.5 %copy-start.40 = (f32[1,512]{1,0:T(1,128)}, f32[1,512]{1,0:T(1,128)S(1)}, u32[]{:S(2)}) copy-start(f32[1,512]{1,0:T(1,128)S(1)} %slice.1108) | copy-start | bytes 6148
  52.4 77.6 %copy-start.41 = (f32[1,512]{1,0:T(1,128)}, f32[1,512]{1,0:T(1,128)S(1)}, u32[]{:S(2)}) copy-start(f32[1,512]{1,0:T(1,128)S(1)} %slice.1115) | copy-start | bytes 6148
  60.5 3.9 %copy-start.9 = (f32[3,3,512]{2,1,0:T(4,128)}, f32[3,3,512]{2,1,0:T(4,128)S(1)}, u32[]{:S(2)}) copy-start(f32[3,3,512]{2,1,0:T(4,128)S(1)} %slice_subtract_fusion.52) | copy-start | bytes 55300
  128.8 1.5 copy-start.46
  129.0 1.5 copy-start.48
  129.0 1.5 copy-start.49
  129.0 1.5 copy-start.50
  129.1 1.6 copy-start.51
  129.1 1.6 copy-start.52
  129.2 1.6 copy-start.53
  129.2 1.6 copy-start.54
  129.2 1.6 copy-start.55
  130.2 1.6 copy-start.1
  130.2 1.5 copy-start.2
  137.4 18.7 %copy-start.42 = (f32[1,512]{1,0:T(1,128)S(1)}, f32[1,512]{1,0:T(1,128)}, u32[]{:S(2)}) copy-start(f32[1,512]{1,0:T(1,128)} %copy-done.41) | copy-start | bytes 6148
  153.2 11.4 %copy-start.32 = (f32[1,512]{1,0:T(1,128)S(1)}, f32[1,512]{1,0:T(1,128)}, u32[]{:S(2)}) copy-start(f32[1,512]{1,0:T(1,128)} %copy-done.31) | copy-start | bytes 6148
  155.0 10.1 %copy-start.30 = (f32[1,512]{1,0:T(1,128)S(1)}, f32[1,512]{1,0:T(1,128)}, u32[]{:S(2)}) copy-start(f32[1,512]{1,0:T(1,128)} %copy-done.29) | copy-start | bytes 6148
  156.1 9.4 %copy-start.28 = (f32[1,512]{1,0:T(1,128)S(1)}, f32[1,512]{1,0:T(1,128)}, u32[]{:S(2)}) copy-start(f32[1,512]{1,0:T(1,128)} %copy-done.27) | copy-start | bytes 6148
  157.4 8.7 %copy-start.26 = (f32[1,512]{1,0:T(1,128)S(1)}, f32[1,512]{1,0:T(1,128)}, u32[]{:S(2)}) copy-start(f32[1,512]{1,0:T(1,128)} %copy-done.25) | copy-start | bytes 6148
  159.2 7.3 %copy-start.24 = (f32[1,512]{1,0:T(1,128)S(1)}, f32[1,512]{1,0:T(1,128)}, u32[]{:S(2)}) copy-start(f32[1,512]{1,0:T(1,128)} %copy-done.23) | copy-start | bytes 6148
  160.4 6.7 %copy-start.22 = (f32[1,512]{1,0:T(1,128)S(1)}, f32[1,512]{1,0:T(1,128)}, u32[]{:S(2)}) copy-start(f32[1,512]{1,0:T(1,128)} %copy-done.21) | copy-start | bytes 6148
  161.5 6.1 %copy-start.20 = (f32[1,512]{1,0:T(1,128)S(1)}, f32[1,512]{1,0:T(1,128)}, u32[]{:S(2)}) copy-start(f32[1,512]{1,0:T(1,128)} %copy-done.19) | copy-start | bytes 6148
  163.4 4.9 %copy-start.18 = (f32[16,32]{1,0:T(8,128)S(1)}, f32[16,32]{1,0:T(8,128)}, u32[]{:S(2)}) copy-start(f32[16,32]{1,0:T(8,128)} %div.867) | copy-start | bytes 6148
  164.9 3.6 %copy-start.16 = (f32[1,2,16,32]{3,2,1,0:T(8,128)S(1)}, f32[1,2,16,32]{3,2,1,0:T(8,128)}, u32[]{:S(2)}) copy-start(f32[1,2,16,32]{3,2,1,0:T(8,128)} %stack.177) | copy-start | bytes 12292
  165.0 3.6 %copy-start.15 = (f32[1,2,16,32]{3,2,1,0:T(8,128)S(1)}, f32[1,2,16,32]{3,2,1,0:T(8,128)}, u32[]{:S(2)}) copy-start(f32[1,2,16,32]{3,2,1,0:T(8,128)} %stack.178) | copy-start | bytes 12292
  165.0 3.6 %copy-start.14 = (f32[1,2,16,32]{3,2,1,0:T(8,128)S(1)}, f32[1,2,16,32]{3,2,1,0:T(8,128)}, u32[]{:S(2)}) copy-start(f32[1,2,16,32]{3,2,1,0:T(8,128)} %stack.179) | copy-start | bytes 12292
  165.1 3.7 %copy-start.13 = (f32[1,2,16,32]{3,2,1,0:T(8,128)S(1)}, f32[1,2,16,32]{3,2,1,0:T(8,128)}, u32[]{:S(2)}) copy-start(f32[1,2,16,32]{3,2,1,0:T(8,128)} %stack.182) | copy-start | bytes 12292
  165.1 3.8 %copy-start.12 = (f32[1,2,16,32]{3,2,1,0:T(8,128)S(1)}, f32[1,2,16,32]{3,2,1,0:T(8,128)}, u32[]{:S(2)}) copy-start(f32[1,2,16,32]{3,2,1,0:T(8,128)} %stack.183) | copy-start | bytes 12292
  165.1 3.7 %copy-start.11 = (f32[1,2,16,32]{3,2,1,0:T(8,128)S(1)}, f32[1,2,16,32]{3,2,1,0:T(8,128)}, u32[]{:S(2)}) copy-start(f32[1,2,16,32]{3,2,1,0:T(8,128)} %stack.184) | copy-start | bytes 12292
  (11 other events, 14.4 us)
Sparse Core Ops, SparseCore 0:
  170.6 79.7 all-gather.1
where the time goes:
time: 268 us; the launch traced here: 267 us
  waiting for transfers between devices  131 us (49%)
  local copies, waits for them, and re-layouts  43.2 us (16%)
  other arithmetic  32.3 us (12%)
  matrix products  18.8 us (7%)
  between operations  17.4 us (6%)
  starting transfers between devices  13.5 us (5%)
  blocking collectives  10.6 us (4%)
    all_gather x1, waiting for transfers between devices, per_device(): lax.all_gather(mode_amplitudes, 'chan', axis=1, tiled=True)  79.9 us
    all_to_all x1, waiting for transfers between devices, per_device(): lax.all_to_all(visibility, 'chan', split_axis=1, concat_axis=0, tiled=True)  50.9 us
    unnamed x28, other arithmetic  14.1 us
    all_to_all x1, starting transfers between devices, per_device(): lax.all_to_all(visibility, 'chan', split_axis=1, concat_axis=0, tiled=True)  13.5 us
    unnamed x577, local copies, waits for them, and re-layouts  11.3 us
    all_gather x1, blocking collectives, per_device(): spectral_templates = lax.all_gather(fit_modes, 'grp', axis=0, tiled=True)  10.6 us
    dot_general x1, matrix products, per_device(): jnp.dot(local_basis, lax.all_gather(mode_amplitudes, 'chan', axis=1, tile...  9.52 us
    mul x2, local copies, waits for them, and re-layouts, solve_amplitudes(): assigned_rows.reshape(channel_count, antenna_pairs_list, 2, sample_values)  7.88 us
  transfers between devices with their start and end apart: 2, of which 2 were waited for; matrix products, arithmetic and copies ran while one was open for 12% of the time, Pallas kernels for 0%

commit v1 on v0

v1 whole, which is shorter than its diff:
```python
import functools

import jax
import jax.numpy as jnp
from jax import lax
from jax.experimental import pallas as pl
from jax.experimental.pallas import tpu as pltpu
from jax.sharding import PartitionSpec as P

MESH = pl.DeviceIdType.MESH
damping = 0.1

NX = 4
NY = 4
NZ = 8
NC = 2
MODES = 32
LANES = 128
ROWS = 16
SLAB = 256
COLS = 1024
HALF = 512
SEL = NY * NC * ROWS
F32 = jnp.float32
BF16 = jnp.bfloat16


def split(value):
    high = value.astype(BF16)
    low = (value - high.astype(F32)).astype(BF16)
    return high, low


def widen(mask):
    lane = lax.broadcasted_iota(jnp.int32, mask.shape, 1)
    by32 = pltpu.roll(mask, 32, 1)
    by64 = pltpu.roll(mask, 64, 1)
    by96 = pltpu.roll(mask, 96, 1)
    first = jnp.where(lane < 32, mask, jnp.where(lane < 96, by32, by64))
    second = jnp.where(lane < 32, by64, jnp.where(lane < 96, by96, mask))
    return jnp.concatenate([first, second], axis=1)


def dot(a, b):
    return lax.dot_general(a, b, (((1,), (0,)), ((), ())), preferred_element_type=F32)


def fit_kernel(
    vis,
    mask,
    modes,
    valid,
    coef,
    table,
    own_mask,
    got_mask,
    got_vis,
    weight,
    gram,
    flipped,
    chosen,
    partial,
    chain,
    answer,
    own_sem,
    table_sem,
    mask_sem,
    vis_sem,
    chain_sem,
    send_sem,
    chain_send,
):
    x = lax.axis_index("grp")
    chan = lax.axis_index("chan")
    y = chan // (NZ * NC)
    z = (chan // NC) % NZ
    core = chan % NC

    def at(yy, zz, cc):
        return (yy * NZ + zz) * NC + cc

    def ahead(steps):
        return (z + steps + NZ) % NZ

    barrier = pltpu.get_barrier_semaphore()
    for step in range(1, NX):
        pl.semaphore_signal(barrier, 1, device_id={"grp": (x + step) % NX}, device_id_type=MESH)
    for step in range(1, NZ):
        pl.semaphore_signal(barrier, 1, device_id={"chan": at(y, ahead(step), core)}, device_id_type=MESH)
    for step in range(1, NY * NC):
        peer = at((y + step // NC) % NY, z, (core + step) % NC)
        pl.semaphore_signal(barrier, 1, device_id={"chan": peer}, device_id_type=MESH)

    mine = y * NC + core
    local_table = pltpu.make_async_copy(modes, table.at[pl.ds(pl.multiple_of(x * SLAB, SLAB), SLAB)], table_sem.at[0])
    local_table.start()
    local_mask = pltpu.make_async_copy(mask, own_mask, own_sem.at[0])
    local_mask.start()
    pltpu.make_async_copy(mask.at[:, z], got_mask.at[z], mask_sem.at[z]).start()
    for zz in range(NZ):
        source = vis.at[:, pl.ds(pl.multiple_of(at(y, zz, core) * COLS, COLS), COLS)]
        pltpu.make_async_copy(
            source, got_vis.at[zz, pl.ds(pl.multiple_of(mine * ROWS, ROWS), ROWS)], vis_sem.at[zz]
        ).start()

    pl.semaphore_wait(barrier, NX - 1 + NZ - 1 + NY * NC - 1)

    for step in range(1, NX):
        pltpu.make_async_remote_copy(
            src_ref=modes,
            dst_ref=table.at[pl.ds(pl.multiple_of(x * SLAB, SLAB), SLAB)],
            send_sem=send_sem.at[0],
            recv_sem=table_sem.at[1],
            device_id={"grp": (x + step) % NX},
            device_id_type=MESH,
        ).start()

    order = (4, 3, -3, 2, -2, 1, -1)
    for steps in order:
        there = ahead(steps)
        pltpu.make_async_remote_copy(
            src_ref=mask.at[:, there],
            dst_ref=got_mask.at[z],
            send_sem=send_sem.at[1],
            recv_sem=mask_sem.at[z],
            device_id={"chan": at(y, there, core)},
            device_id_type=MESH,
        ).start()
    for steps in order + (0,):
        owner = ahead(steps)
        for step in range(1, NY * NC):
            yy = (y + step // NC) % NY
            cc = (core + step) % NC
            source = vis.at[:, pl.ds(pl.multiple_of(at(yy, owner, cc) * COLS, COLS), COLS)]
            pltpu.make_async_remote_copy(
                src_ref=source,
                dst_ref=got_vis.at[owner, pl.ds(pl.multiple_of(mine * ROWS, ROWS), ROWS)],
                send_sem=send_sem.at[2],
                recv_sem=vis_sem.at[owner],
                device_id={"chan": at(yy, z, cc)},
                device_id_type=MESH,
            ).start()

    local_mask.wait()

    @pl.loop(0, NY * NZ)
    def _(block):
        yy = block // NZ
        zz = block % NZ
        for group in range(HALF // LANES):
            kept = 1 - own_mask[yy, zz, :, group * LANES : (group + 1) * LANES]
            weight[
                pl.ds(pl.multiple_of(block * 32, 32), 32), group * 2 * LANES : (group + 1) * 2 * LANES
            ] = widen(kept.astype(F32)).astype(BF16)

    local_table.wait()
    others = table.at[pl.ds(0, (NX - 1) * SLAB)]
    pltpu.make_async_copy(others, others, table_sem.at[1]).wait()
    flipped[...] = jnp.transpose(table[...])[:MODES]
    rows = [
        table[pl.ds(pl.multiple_of(yy * SLAB + z * NC * ROWS, 32), NC * ROWS), :] for yy in range(NY)
    ]
    high, low = split(jnp.transpose(jnp.concatenate(rows, axis=0))[:MODES])
    chosen[...] = jnp.concatenate([high, high, low], axis=1)

    eye_row = lax.broadcasted_iota(jnp.int32, (MODES, COLS), 0)
    inside = valid[...]

    @pl.loop(0, MODES // 4)
    def _(block):
        pairs = [flipped[...] * flipped[pl.ds(block * 4 + k, 1), :] for k in range(4)]
        high, low = split(jnp.concatenate(pairs, axis=0))
        for part in range(COLS // 256):
            cols = slice(part * 256, (part + 1) * 256)
            held = weight[:, cols]
            sums = (dot(high, held) + dot(low, held)) * inside[:, cols]
            for k in range(4):
                ridge = jnp.where(eye_row[:, cols] == block * 4 + k, damping, 0.0)
                gram[block * 4 + k, :, cols] = sums[k * MODES : (k + 1) * MODES] + ridge

    @pl.loop(0, MODES)
    def _(k):
        scale = lax.rsqrt(gram[k, pl.ds(k, 1), :])
        column = jnp.where(eye_row >= k, gram[k] * scale, 0.0)
        gram[k] = column

        @pl.loop(k + 1, MODES)
        def _(j):
            gram[j] = gram[j] - gram[k] * gram[k, pl.ds(j, 1), :]

    def project(owner, out):
        pltpu.make_async_copy(got_mask.at[owner], got_mask.at[owner], mask_sem.at[owner]).wait()
        pltpu.make_async_copy(got_vis.at[owner], got_vis.at[owner], vis_sem.at[owner]).wait()

        @pl.loop(0, HALF // LANES)
        def _(group):
            narrow = pl.ds(pl.multiple_of(group * LANES, LANES), LANES)
            wide = pl.ds(pl.multiple_of(group * 2 * LANES, 2 * LANES), 2 * LANES)
            flags = jnp.concatenate([got_mask[owner, yy, :, narrow] for yy in range(NY)], axis=0)
            kept = widen((1 - flags).astype(F32))
            high, low = split(kept * got_vis[owner, :, wide])
            out[:, wide] = dot(chosen[...], jnp.concatenate([high, low, high], axis=0))

    def send(way, slot, rows):
        return pltpu.make_async_remote_copy(
            src_ref=partial.at[way, slot, rows],
            dst_ref=chain.at[way, slot, rows],
            send_sem=chain_send.at[way, slot],
            recv_sem=chain_sem.at[way, slot],
            device_id={"chan": at(y, ahead(1 - 2 * way), core)},
            device_id_type=MESH,
        )

    upper = pl.ds(0, MODES // 2)
    lower = pl.ds(MODES // 2, MODES // 2)
    project(ahead(4), partial.at[0, 0])
    partial[1, 0, MODES // 2 :] = partial[0, 0, MODES // 2 :]
    sends = [send(0, 0, upper), send(1, 0, lower)]
    for s in sends:
        s.start()
    everything = pl.ds(0, MODES)
    for slot in range(1, 4):
        for way in range(2):
            project(ahead((4 - slot) * (1 - 2 * way)), partial.at[way, slot])
            if slot == 1:
                piece = (upper, lower)[way]
                sends[way].wait_recv()
                partial[way, slot, piece] = partial[way, slot, piece] + chain[way, 0, piece]
            else:
                sends[(slot - 1) * 2 + way].wait_recv()
                partial[way, slot] = partial[way, slot] + chain[way, slot - 1]
            out = send(way, slot, everything)
            out.start()
            sends.append(out)
    project(z, answer)
    sends[6].wait_recv()
    sends[7].wait_recv()
    answer[...] = (answer[...] + chain[0, 3] + chain[1, 3]) * inside

    @pl.loop(0, MODES)
    def _(k):
        column = gram[k]
        row = answer[pl.ds(k, 1), :] / gram[k, pl.ds(k, 1), :]
        answer[...] = answer[...] - jnp.where(eye_row > k, column * row, 0.0)
        answer[pl.ds(k, 1), :] = row

    coef[...] = jnp.zeros_like(coef)

    @pl.loop(0, MODES)
    def _(step):
        k = MODES - 1 - step
        later = jnp.sum(gram[k] * coef[...], axis=0, keepdims=True)
        coef[pl.ds(k, 1), :] = (answer[pl.ds(k, 1), :] - later) / gram[k, pl.ds(k, 1), :]

    for s in sends:
        s.wait_send()
    sent = table.at[pl.ds(0, (NX - 1) * SLAB)]
    pltpu.make_async_copy(sent, sent, send_sem.at[0]).wait()
    sent = got_mask.at[pl.ds(0, NZ - 1)]
    pltpu.make_async_copy(sent, sent, send_sem.at[1]).wait()
    sent = got_vis.at[pl.ds(0, NY * NC - 1)]
    pltpu.make_async_copy(sent, sent, send_sem.at[2]).wait()


def fit(vis, mask, modes, valid):
    anywhere = pl.BlockSpec(memory_space=pl.ANY)
    held = pl.BlockSpec(memory_space=pltpu.VMEM)
    return pl.pallas_call(
        fit_kernel,
        out_shape=(
            jax.ShapeDtypeStruct((MODES, COLS), F32),
            jax.ShapeDtypeStruct((NX * SLAB, LANES), F32),
        ),
        in_specs=[anywhere, anywhere, anywhere, held],
        out_specs=(held, held),
        scratch_shapes=[
            pltpu.VMEM((NY, NZ, NC * ROWS, HALF), jnp.int32),
            pltpu.VMEM((NZ, NY, NC * ROWS, HALF), jnp.int32),
            pltpu.VMEM((NZ, SEL, COLS), F32),
            pltpu.VMEM((NX * SLAB, COLS), BF16),
            pltpu.VMEM((MODES, MODES, COLS), F32),
            pltpu.VMEM((MODES, NX * SLAB), F32),
            pltpu.VMEM((MODES, 3 * SEL), BF16),
            pltpu.VMEM((2, 4, MODES, COLS), F32),
            pltpu.VMEM((2, 4, MODES, COLS), F32),
            pltpu.VMEM((MODES, COLS), F32),
            pltpu.SemaphoreType.DMA((1,)),
            pltpu.SemaphoreType.DMA((2,)),
            pltpu.SemaphoreType.DMA((NZ,)),
            pltpu.SemaphoreType.DMA((NZ,)),
            pltpu.SemaphoreType.DMA((2, 4)),
            pltpu.SemaphoreType.DMA((3,)),
            pltpu.SemaphoreType.DMA((2, 4)),
        ],
        compiler_params=pltpu.CompilerParams(
            collective_id=0, has_side_effects=True, vmem_limit_bytes=60 * 1024 * 1024
        ),
        name="fit",
    )(vis, mask, modes, valid)


def per_device(visibility, interference_mask, valid_time_count, fit_modes):
    owned = valid_time_count.shape[0]
    times = HALF // owned
    inside = lax.broadcasted_iota(jnp.int32, (owned, 2, times), 2) < valid_time_count[:, None, None]
    valid = inside.astype(F32).reshape(1, COLS)
    modes = jnp.pad(fit_modes, ((0, 0), (0, LANES - MODES)))
    mask = interference_mask.reshape(NY, NZ, NC * ROWS, HALF)
    coef, table = fit(visibility, mask, modes, valid)
    local_rows = visibility.shape[0]
    local_basis = lax.dynamic_slice_in_dim(
        table, lax.axis_index("chan") * local_rows, local_rows, 0
    )[:, :MODES]
    model = jnp.dot(
        local_basis,
        lax.all_gather(coef, "chan", axis=1, tiled=True),
        precision=lax.Precision.HIGHEST,
        preferred_element_type=F32,
    )
    return visibility - model


def solution(mesh):
    placed = (P("chan", "grp"), P(None, ("grp", "chan")), P(("grp", "chan")), P("grp", None))
    return jax.shard_map(
        per_device, mesh=mesh, in_specs=placed, out_specs=P("chan", "grp"), check_vma=False
    )
```

time: 268 us -> 181 us (0.68)
  Pallas kernels: 0 us -> 72 us
  waiting for transfers between devices: 131 us -> 84.3 us
  local copies, waits for them, and re-layouts: 43.2 us -> 2.21 us
  other arithmetic: 32.3 us -> 0.73 us
  starting transfers between devices: 13.5 us -> 0.01 us
  blocking collectives: 10.6 us -> 0 us
  matrix products: 18.8 us -> 8.4 us
  between operations: 17.4 us -> 13.4 us
    pallas_call x0 -> x1, Pallas kernels: none -> 72 us  [fit(): pl.pallas_call(fit_kernel, out_shape=(jax.ShapeDtypeStruct((MODES, COLS),...]
    all_to_all x1 -> x0, waiting for transfers between devices: 50.9 us -> none  [per_device(): lax.all_to_all(visibility, 'chan', split_axis=1, concat_axis=0, tiled=True)]
    unnamed x28 -> x0, other arithmetic: 14.1 us -> none
    all_to_all x1 -> x0, starting transfers between devices: 13.5 us -> none  [per_device(): lax.all_to_all(visibility, 'chan', split_axis=1, concat_axis=0, tiled=True)]
    all_gather x1 -> x0, blocking collectives: 10.6 us -> none  [per_device(): spectral_templates = lax.all_gather(fit_modes, 'grp', axis=0, tiled=True)]
    dot_general x3 -> x1, matrix products: 18.8 us -> 8.4 us  [per_device(): jnp.dot(local_basis, lax.all_gather(coef, 'chan', axis=1, tiled=True), pr...]
    unnamed x577 -> x1, local copies, waits for them, and re-layouts: 11.3 us -> 0.85 us
    slice x95 -> x0, local copies, waits for them, and re-layouts: 8.62 us -> none  [the longest x32 7.51 us: solve_normal(): current = remains[0] / column[0][None, :]]
  transfers between devices with their start and end apart: 2 -> 1, of which waited for: 2 -> 1; matrix products, arithmetic and copies ran while one was open for 12% -> 0% of each run, Pallas kernels for 0% -> 0%
where the time goes in v1:
time: 181 us
  waiting for transfers between devices  84.3 us (47%)
  Pallas kernels  72 us (40%)
  between operations  13.4 us (7%)
  matrix products  8.4 us (5%)
  local copies, waits for them, and re-layouts  2.21 us (1%)
    all_gather x1, waiting for transfers between devices, per_device(): lax.all_gather(coef, 'chan', axis=1, tiled=True)  84.3 us
    pallas_call x1, Pallas kernels, fit(): pl.pallas_call(fit_kernel, out_shape=(jax.ShapeDtypeStruct((MODES, COLS),...  72 us
    dot_general x1, matrix products, per_device(): jnp.dot(local_basis, lax.all_gather(coef, 'chan', axis=1, tiled=True), pr...  8.4 us
  transfers between devices with their start and end apart: 1, of which 1 were waited for; matrix products, arithmetic and copies ran while one was open for 0% of the time, Pallas kernels for 0%

profile of v1, /device:TPU:1, one launch (start us, length us, event | category | flops | bytes accessed | tf_op | source)
XLA Modules:
  0.0 181.1 jit_solution(8794615860581392287)
XLA Ops:
  6.5 0.0 all-gather.2.cloned.1.call-start
  6.5 0.7 compare_convert_fusion
  7.3 0.7 reshape.33.valid
  8.0 0.9 copy.5
  8.8 0.7 pad.4.modes
  9.5 72.0 %fit.1 = (f32[32,1024]{1,0:T(8,128)}, f32[1024,128]{1,0:T(8,128)}) custom-call(f32[16,65536]{1,0:T(8,128)} %vis.1, s32[4,8,32,512]{3,2,1,0:T(8,128)} %bitcast.2, f32[256,128]{1,0:T(8,128)} %pad.4.modes, f32[1,1024]{1,0:T(1,128)} %reshape.33.valid), custom_call_target="tpu_custom_call" | custom-call | tf_op jit(solution)/shard_map/fit/pallas_call | solution.py:268
  81.5 0.0 all-gather.2.cloned.1.call-update
  81.6 84.3 %all-gather.2.cloned.1.call-done = f32[32,65536]{1,0:T(8,128)} async-done(((f32[32,1024]{1,0:T(8,128)}), f32[32,65536]{1,0:T(8,128)}) %all-gather.2.cloned.1.call-update) | async-done | bytes 8388624 | tf_op jit(solution)/shard_map/all_gather | solution.py:316
  165.9 8.4 %convolution_subtract_fusion = f32[16,65536]{1,0:T(8,128)} fusion(f32[16,65536]{1,0:T(8,128)} %vis.1, f32[32,65536]{1,0:T(8,128)} %all-gather.2.cloned.1.call-done, f32[1024,128]{1,0:T(8,128)} %get-tuple-element.7, s32[]{:T(128)S(6)} %select_n.3), kind=kOutput, calls=%fused_computation | convolution fusion | flops 403701760 | bytes 16785412 | tf_op jit(solution)/shard_map/dot_general | solution.py:314
Async XLA Ops:
  6.5 159.3 %all-gather.2.cloned.1.call-start = ((), (), s32[]{:S(2)}) async-start(), calls=%async_computation | async-start | bytes 8519680 | tf_op jit(solution)/shard_map/all_gather | solution.py:316
Sparse Core Ops, SparseCore 0:
  81.7 84.1 all-gather.1

commit v2 on v1

--- a/solution.py
+++ b/solution.py
@@ -21,6 +21,9 @@
 COLS = 1024
 HALF = 512
 SEL = NY * NC * ROWS
+FIRST, SECOND = slice(0, 512), slice(512, 1024)
+FIRST_OF = slice(0, 256), slice(256, 512)
+SECOND_OF = slice(512, 768), slice(768, 1024)
 F32 = jnp.float32
 BF16 = jnp.bfloat16
 
@@ -50,7 +53,10 @@
     mask,
     modes,
     valid,
-    coef,
+    out,
+    coefs,
+    basis,
+    kept_vis,
     table,
     own_mask,
     got_mask,
@@ -69,6 +75,15 @@
     chain_sem,
     send_sem,
     chain_send,
+    across_sem,
+    along_sem,
+    first_sem,
+    spread_sem,
+    twin_sem,
+    load_sem,
+    store_sem,
+    link_send,
+    twin_send,
 ):
     x = lax.axis_index("grp")
     chan = lax.axis_index("chan")
@@ -141,6 +156,11 @@
                 device_id_type=MESH,
             ).start()
 
+    @pl.loop(0, NY * NZ * NC)
+    def _(block):
+        source = vis.at[:, pl.ds(pl.multiple_of(block * COLS, COLS), COLS)]
+        pltpu.make_async_copy(source, kept_vis.at[block], load_sem.at[0]).start()
+
     local_mask.wait()
 
     @pl.loop(0, NY * NZ)
@@ -162,6 +182,9 @@
     ]
     high, low = split(jnp.transpose(jnp.concatenate(rows, axis=0))[:MODES])
     chosen[...] = jnp.concatenate([high, high, low], axis=1)
+
+    high, low = split(table[pl.ds(pl.multiple_of(chan * ROWS, ROWS), ROWS), :][:, :MODES])
+    basis[...] = jnp.concatenate([high, high, low], axis=1)
 
     eye_row = lax.broadcasted_iota(jnp.int32, (MODES, COLS), 0)
     inside = valid[...]
@@ -229,9 +252,8 @@
             else:
                 sends[(slot - 1) * 2 + way].wait_recv()
                 partial[way, slot] = partial[way, slot] + chain[way, slot - 1]
-            out = send(way, slot, everything)
-            out.start()
-            sends.append(out)
+            sends.append(send(way, slot, everything))
+            sends[-1].start()
     project(z, answer)
     sends[6].wait_recv()
     sends[7].wait_recv()
@@ -244,7 +266,8 @@
         answer[...] = answer[...] - jnp.where(eye_row > k, column * row, 0.0)
         answer[pl.ds(k, 1), :] = row
 
-    coef[...] = jnp.zeros_like(coef)
+    coef = coefs.at[y, z, core]
+    coef[...] = jnp.zeros((MODES, COLS), F32)
 
     @pl.loop(0, MODES)
     def _(step):
@@ -252,6 +275,165 @@
         later = jnp.sum(gram[k] * coef[...], axis=0, keepdims=True)
         coef[pl.ds(k, 1), :] = (answer[pl.ds(k, 1), :] - later) / gram[k, pl.ds(k, 1), :]
 
+    pltpu.make_async_copy(kept_vis, kept_vis, load_sem.at[0]).wait()
+
+    def push(piece, peer, arrived, sent=None):
+        pltpu.make_async_remote_copy(
+            src_ref=piece,
+            dst_ref=piece,
+            send_sem=link_send.at[0] if sent is None else sent,
+            recv_sem=arrived,
+            device_id={"chan": peer},
+            device_id_type=MESH,
+        ).start()
+
+    def wait(piece, arrived):
+        pltpu.make_async_copy(piece, piece, arrived).wait()
+
+    def beside(way):
+        return at(y, ahead(1 - 2 * way), core)
+
+    def finish(yy, zz, cc, half):
+        cols = (FIRST, SECOND)[half]
+        block = at(yy, zz, cc)
+        high, low = split(coefs[yy, zz, cc, :, cols])
+        model = dot(basis[...], jnp.concatenate([high, low, high], axis=0))
+        kept_vis[block, :, cols] = kept_vis[block, :, cols] - model
+        start = pl.multiple_of(block * COLS + cols.start, LANES)
+        pltpu.make_async_copy(
+            kept_vis.at[block, :, cols], out.at[:, pl.ds(start, cols.stop - cols.start)], store_sem.at[0]
+        ).start()
+
+    def hand(half, yy, zz):
+        cols = (FIRST, SECOND)[half]
+        push(coefs.at[yy, zz, core, :, cols], at(y, z, 1 - core), twin_sem.at[half, yy, zz], twin_send.at[0])
+
+    def take(half, yy, zz):
+        wait(coefs.at[yy, zz, 1 - core, :, (FIRST, SECOND)[half]], twin_sem.at[half, yy, zz])
+        finish(yy, zz, 1 - core, half)
+
+    def along(yy, zz, way, far):
+        if far < 4:
+            push(coefs.at[yy, zz, core, :, FIRST], beside(way), along_sem.at[way, far, yy])
+        elif far == 4:
+            push(coefs.at[yy, zz, core, :, FIRST_OF[way]], beside(way), along_sem.at[way, far, yy])
+
+    def first(zz, way, far):
+        if far < 4:
+            push(coefs.at[y, zz, core, :, SECOND], beside(way), first_sem.at[way, far])
+        elif far == 4:
+            push(coefs.at[y, zz, core, :, SECOND_OF[way]], beside(way), first_sem.at[way, far])
+
+    def spread(zz):
+        for step in (1, 3, 2):
+            push(coefs.at[y, zz, core, :, SECOND], at((y + step) % NY, z, core), spread_sem.at[y, zz])
+
+    for way in range(2):
+        first(z, way, 1)
+    for step in (1, 3, 2):
+        push(coefs.at[y, z, core, :, FIRST], at((y + step) % NY, z, core), across_sem.at[y])
+    for way in range(2):
+        along(y, z, way, 1)
+    spread(z)
+    hand(0, y, z)
+    hand(1, y, z)
+    finish(y, z, core, 0)
+    finish(y, z, core, 1)
+
+    def origin(way, far):
+        return ahead(far * (2 * way - 1))
+
+    def second_of(far):
+        if far == 4:
+            zz = ahead(4)
+            for way in range(2):
+                wait(coefs.at[y, zz, core, :, SECOND_OF[way]], first_sem.at[way, 4])
+            spread(zz)
+            hand(1, y, zz)
+            finish(y, zz, core, 1)
+            return
+        for way in range(2):
+            zz = origin(way, far)
+            wait(coefs.at[y, zz, core, :, SECOND], first_sem.at[way, far])
+            first(zz, way, far + 1)
+            spread(zz)
+            hand(1, y, zz)
+        for way in range(2):
+            finish(y, origin(way, far), core, 1)
+
+    def second_spread(far):
+        @pl.loop(1, NY)
+        def _(step):
+            yy = (y + step) % NY
+            for zz in (z,) if far == 0 else (ahead(4),) if far == 4 else (ahead(far), ahead(-far)):
+                wait(coefs.at[yy, zz, core, :, SECOND], spread_sem.at[yy, zz])
+                hand(1, yy, zz)
+                finish(yy, zz, core, 1)
+
+    def first_across():
+        @pl.loop(1, NY)
+        def _(step):
+            yy = (y + step) % NY
+            wait(coefs.at[yy, z, core, :, FIRST], across_sem.at[yy])
+            for way in range(2):
+                along(yy, z, way, 1)
+            hand(0, yy, z)
+            finish(yy, z, core, 0)
+
+    def first_of(far):
+        @pl.loop(0, NY)
+        def _(step):
+            yy = (y + step) % NY
+            if far == 4:
+                zz = ahead(4)
+                for way in range(2):
+                    wait(coefs.at[yy, zz, core, :, FIRST_OF[way]], along_sem.at[way, 4, yy])
+                hand(0, yy, zz)
+                finish(yy, zz, core, 0)
+                return
+            for way in range(2):
+                zz = origin(way, far)
+                wait(coefs.at[yy, zz, core, :, FIRST], along_sem.at[way, far, yy])
+                along(yy, zz, way, far + 1)
+                hand(0, yy, zz)
+            for way in range(2):
+                finish(yy, origin(way, far), core, 0)
+
+    def taken(half, far):
+        @pl.loop(0, NY)
+        def _(step):
+            yy = (y + step) % NY
+            for zz in (z,) if far == 0 else (ahead(4),) if far == 4 else (ahead(far), ahead(-far)):
+                take(half, yy, zz)
+
+    second_of(1)
+    first_across()
+    second_spread(0)
+    second_of(2)
+    first_of(1)
+    taken(0, 0)
+    taken(1, 0)
+    second_spread(1)
+    second_of(3)
+    first_of(2)
+    taken(0, 1)
+    taken(1, 1)
+    second_spread(2)
+    second_of(4)
+    first_of(3)
+    taken(0, 2)
+    taken(1, 2)
+    second_spread(3)
+    first_of(4)
+    second_spread(4)
+    taken(0, 3)
+    taken(1, 3)
+    taken(0, 4)
+    taken(1, 4)
+
+    pltpu.make_async_copy(kept_vis, kept_vis, store_sem.at[0]).wait()
+    pltpu.make_async_copy(gram.at[: MODES - 1], gram.at[: MODES - 1], link_send.at[0]).wait()
+    pltpu.make_async_copy(gram, gram, twin_send.at[0]).wait()
     for s in sends:
         s.wait_send()
     sent = table.at[pl.ds(0, (NX - 1) * SLAB)]
@@ -267,13 +449,14 @@
     held = pl.BlockSpec(memory_space=pltpu.VMEM)
     return pl.pallas_call(
         fit_kernel,
-        out_shape=(
-            jax.ShapeDtypeStruct((MODES, COLS), F32),
-            jax.ShapeDtypeStruct((NX * SLAB, LANES), F32),
-        ),
+        out_shape=jax.ShapeDtypeStruct(vis.shape, F32),
         in_specs=[anywhere, anywhere, anywhere, held],
-        out_specs=(held, held),
+        out_specs=anywhere,
         scratch_shapes=[
+            pltpu.VMEM((NY, NZ, NC, MODES, COLS), F32),
+            pltpu.VMEM((ROWS, 3 * MODES), BF16),
+            pltpu.VMEM((NY * NZ * NC, ROWS, COLS), F32),
+            pltpu.VMEM((NX * SLAB, LANES), F32),
             pltpu.VMEM((NY, NZ, NC * ROWS, HALF), jnp.int32),
             pltpu.VMEM((NZ, NY, NC * ROWS, HALF), jnp.int32),
             pltpu.VMEM((NZ, SEL, COLS), F32),
@@ -291,6 +474,15 @@
             pltpu.SemaphoreType.DMA((2, 4)),
             pltpu.SemaphoreType.DMA((3,)),
             pltpu.SemaphoreType.DMA((2, 4)),
+            pltpu.SemaphoreType.DMA((NY,)),
+            pltpu.SemaphoreType.DMA((2, 5, NY)),
+            pltpu.SemaphoreType.DMA((2, 5)),
+            pltpu.SemaphoreType.DMA((NY, NZ)),
+            pltpu.SemaphoreType.DMA((2, NY, NZ)),
+            pltpu.SemaphoreType.DMA((1,)),
+            pltpu.SemaphoreType.DMA((1,)),
+            pltpu.SemaphoreType.DMA((1,)),
+            pltpu.SemaphoreType.DMA((1,)),
         ],
         compiler_params=pltpu.CompilerParams(
             collective_id=0, has_side_effects=True, vmem_limit_bytes=60 * 1024 * 1024
@@ -306,18 +498,7 @@
     valid = inside.astype(F32).reshape(1, COLS)
     modes = jnp.pad(fit_modes, ((0, 0), (0, LANES - MODES)))
     mask = interference_mask.reshape(NY, NZ, NC * ROWS, HALF)
-    coef, table = fit(visibility, mask, modes, valid)
-    local_rows = visibility.shape[0]
-    local_basis = lax.dynamic_slice_in_dim(
-        table, lax.axis_index("chan") * local_rows, local_rows, 0
-    )[:, :MODES]
-    model = jnp.dot(
-        local_basis,
-        lax.all_gather(coef, "chan", axis=1, tiled=True),
-        precision=lax.Precision.HIGHEST,
-        preferred_element_type=F32,
-    )
-    return visibility - model
+    return fit(visibility, mask, modes, valid)
 
 
 def solution(mesh):

time: 181 us -> 115 us (0.64)
  waiting for transfers between devices: 84.3 us -> 0 us
  Pallas kernels: 72 us -> 107 us
  between operations: 13.4 us -> 0.02 us
  matrix products: 8.4 us -> 0 us
  local copies, waits for them, and re-layouts: 2.21 us -> 6.68 us
    all_gather x1 -> x0, waiting for transfers between devices: 84.3 us -> none  [per_device(): lax.all_gather(coef, 'chan', axis=1, tiled=True)]
    pallas_call x1, Pallas kernels: 72 us -> 107 us  [fit(): pl.pallas_call(fit_kernel, out_shape=jax.ShapeDtypeStruct(vis.shape, F32)...]
    dot_general x1 -> x0, matrix products: 8.4 us -> none  [per_device(): jnp.dot(local_basis, lax.all_gather(coef, 'chan', axis=1, tiled=True), pr...]
    unnamed x1 -> x2, local copies, waits for them, and re-layouts: 0.85 us -> 5.32 us
  transfers between devices with their start and end apart: 1 -> 0, of which waited for: 1 -> 0; matrix products, arithmetic and copies ran while one was open for 0% -> 0% of each run, Pallas kernels for 0% -> 0%
where the time goes in v2:
time: 115 us; the launch traced here: 114 us
  Pallas kernels  107 us (93%)
  local copies, waits for them, and re-layouts  6.68 us (6%)
    pallas_call x1, Pallas kernels, fit(): pl.pallas_call(fit_kernel, out_shape=jax.ShapeDtypeStruct(vis.shape, F32)...  107 us
    unnamed x2, local copies, waits for them, and re-layouts  5.32 us

profile of v2, /device:TPU:1, one launch (start us, length us, event | category | flops | bytes accessed | tf_op | source)
XLA Modules:
  0.0 114.4 jit_solution(15010935033306921138)
XLA Ops:
  0.0 0.7 compare_convert_fusion
  0.7 0.7 reshape.33.valid
  1.4 0.9 copy.5
  2.3 0.7 pad.4.modes
  3.0 107.0 %fit.1 = f32[16,65536]{1,0:T(8,128)} custom-call(f32[16,65536]{1,0:T(8,128)} %vis.1, s32[4,8,32,512]{3,2,1,0:T(8,128)} %bitcast.1, f32[256,128]{1,0:T(8,128)} %pad.4.modes, f32[1,1024]{1,0:T(1,128)} %reshape.33.valid), custom_call_target="tpu_custom_call" | custom-call | tf_op jit(solution)/shard_map/fit/pallas_call | solution.py:450
  110.0 4.5 %copy.7 = f32[16,65536]{1,0:T(8,128)} copy(f32[16,65536]{1,0:T(8,128)} %fit.1) | data formatting | bytes 8388608

commit v3 on v2

v3 whole, which is shorter than its diff:
```python
import functools

import jax
import jax.numpy as jnp
from jax import lax
from jax.experimental import pallas as pl
from jax.experimental.pallas import tpu as pltpu
from jax.sharding import PartitionSpec as P

MESH = pl.DeviceIdType.MESH
damping = 0.1

NX = 4
NY = 4
NZ = 8
NC = 2
MODES = 32
LANES = 128
ROWS = 16
SLAB = 256
TIMES = 32
COLS = 1024
HALF = 512
SEL = NY * NC * ROWS
SECOND, FIRST = slice(0, 768), slice(768, 1024)
TURNS = SECOND, FIRST
SECOND_OF = slice(0, 384), slice(384, 768)
F32 = jnp.float32
BF16 = jnp.bfloat16


def split(value):
    high = value.astype(BF16)
    low = (value - high.astype(F32)).astype(BF16)
    return high, low


def widen(mask):
    lane = lax.broadcasted_iota(jnp.int32, mask.shape, 1)
    by32 = pltpu.roll(mask, 32, 1)
    by64 = pltpu.roll(mask, 64, 1)
    by96 = pltpu.roll(mask, 96, 1)
    first = jnp.where(lane < 32, mask, jnp.where(lane < 96, by32, by64))
    second = jnp.where(lane < 32, by64, jnp.where(lane < 96, by96, mask))
    return jnp.concatenate([first, second], axis=1)


def dot(a, b):
    return lax.dot_general(a, b, (((1,), (0,)), ((), ())), preferred_element_type=F32)


def fit_kernel(
    vis,
    mask,
    modes,
    counts,
    out,
    valid,
    coefs,
    basis,
    kept_vis,
    table,
    got_mask,
    got_vis,
    weight,
    gram,
    flipped,
    chosen,
    partial,
    chain,
    answer,
    table_sem,
    mask_sem,
    vis_sem,
    chain_sem,
    send_sem,
    chain_send,
    across_sem,
    along_sem,
    first_sem,
    spread_sem,
    relay_sem,
    twin_sem,
    load_sem,
    link_send,
    twin_send,
):
    x = lax.axis_index("grp")
    chan = lax.axis_index("chan")
    y = chan // (NZ * NC)
    z = (chan // NC) % NZ
    core = chan % NC

    def at(yy, zz, cc):
        return (yy * NZ + zz) * NC + cc

    def ahead(steps):
        return (z + steps + NZ) % NZ

    barrier = pltpu.get_barrier_semaphore()
    for step in range(1, NX):
        pl.semaphore_signal(barrier, 1, device_id={"grp": (x + step) % NX}, device_id_type=MESH)
    for step in range(1, NZ):
        pl.semaphore_signal(barrier, 1, device_id={"chan": at(y, ahead(step), core)}, device_id_type=MESH)
    for step in range(1, NY * NC):
        peer = at((y + step // NC) % NY, z, (core + step) % NC)
        pl.semaphore_signal(barrier, 1, device_id={"chan": peer}, device_id_type=MESH)

    mine = y * NC + core
    flipped[:, pl.ds(pl.multiple_of(x * SLAB, SLAB), SLAB)] = modes[...]
    got_mask[z] = mask[:, z]
    for turn, cols in enumerate(TURNS):
        for zz in range(NZ):
            start = pl.multiple_of(at(y, zz, core) * COLS + cols.start, LANES)
            pltpu.make_async_copy(
                vis.at[:, pl.ds(start, cols.stop - cols.start)],
                got_vis.at[zz, pl.ds(pl.multiple_of(mine * ROWS, ROWS), ROWS), cols],
                vis_sem.at[turn, zz],
            ).start()

    pl.semaphore_wait(barrier, NX - 1 + NZ - 1 + NY * NC - 1)

    for step in range(1, NX):
        pltpu.make_async_remote_copy(
            src_ref=modes,
            dst_ref=flipped.at[:, pl.ds(pl.multiple_of(x * SLAB, SLAB), SLAB)],
            send_sem=send_sem.at[0],
            recv_sem=table_sem.at[0],
            device_id={"grp": (x + step) % NX},
            device_id_type=MESH,
        ).start()

    def send_mask(turn, *distances):
        cols = slice(TURNS[turn].start // 2, TURNS[turn].stop // 2)
        for steps in distances:
            there = ahead(steps)
            pltpu.make_async_remote_copy(
                src_ref=mask.at[:, there, :, cols],
                dst_ref=got_mask.at[z, :, :, cols],
                send_sem=send_sem.at[1],
                recv_sem=mask_sem.at[turn, z],
                device_id={"chan": at(y, there, core)},
                device_id_type=MESH,
            ).start()

    def send_vis():
        for turn, cols in enumerate(TURNS):
            for steps in (4, 3, -3, 2, -2, 1, -1, 0):
                owner = ahead(steps)
                for step in range(1, NY * NC):
                    yy = (y + step // NC) % NY
                    cc = (core + step) % NC
                    start = pl.multiple_of(at(yy, owner, cc) * COLS + cols.start, LANES)
                    pltpu.make_async_remote_copy(
                        src_ref=vis.at[:, pl.ds(start, cols.stop - cols.start)],
                        dst_ref=got_vis.at[owner, pl.ds(pl.multiple_of(mine * ROWS, ROWS), ROWS), cols],
                        send_sem=send_sem.at[2],
                        recv_sem=vis_sem.at[turn, owner],
                        device_id={"chan": at(yy, z, cc)},
                        device_id_type=MESH,
                    ).start()

        @pl.loop(0, NY * NZ * NC)
        def _(block):
            source = vis.at[:, pl.ds(pl.multiple_of(block * COLS, COLS), COLS)]
            pltpu.make_async_copy(source, kept_vis.at[block], load_sem.at[0]).start()

    eye_row = lax.broadcasted_iota(jnp.int32, (MODES, COLS), 0)

    def weigh():
        @pl.loop(0, NY * NZ)
        def _(block):
            yy = block // NZ
            zz = block % NZ
            for group in range(HALF // LANES):
                kept = 1 - mask[yy, zz, :, group * LANES : (group + 1) * LANES]
                weight[
                    pl.ds(pl.multiple_of(block * 32, 32), 32), group * 2 * LANES : (group + 1) * 2 * LANES
                ] = widen(kept.astype(F32)).astype(BF16)

        others = flipped.at[:, pl.ds(0, (NX - 1) * SLAB)]
        pltpu.make_async_copy(others, others, table_sem.at[0]).wait()
        filler = jnp.zeros((LANES - MODES, NX * SLAB), F32)
        table[...] = jnp.transpose(jnp.concatenate([flipped[...], filler], axis=0))
        rows = [
            table[pl.ds(pl.multiple_of(yy * SLAB + z * NC * ROWS, 32), NC * ROWS), :] for yy in range(NY)
        ]
        high, low = split(jnp.transpose(jnp.concatenate(rows, axis=0))[:MODES])
        chosen[...] = jnp.concatenate([high, high, low], axis=1)

        high, low = split(table[pl.ds(pl.multiple_of(chan * ROWS, ROWS), ROWS), :][:, :MODES])
        basis[...] = jnp.concatenate([high, high, low], axis=1)

    def make_gram():
        column = lax.broadcasted_iota(jnp.int32, (2 * LANES, COLS), 1)
        owner = lax.broadcasted_iota(jnp.int32, (2 * LANES, COLS), 0)
        picked = jnp.where(column // TIMES // 2 == owner, 1.0, 0.0).astype(BF16)
        filler = jnp.zeros((8, 2 * LANES - counts.shape[1]), F32)
        count = jnp.concatenate([jnp.broadcast_to(counts[...].astype(F32), (8, counts.shape[1])), filler], axis=1)
        count = dot(count.astype(BF16), picked)[:1]
        times = lax.broadcasted_iota(jnp.int32, (1, COLS), 1) % TIMES
        valid[...] = jnp.where(times.astype(F32) < count, 1.0, 0.0)
        inside = valid[...]

        @pl.loop(0, MODES // 4)
        def _(block):
            pairs = [flipped[...] * flipped[pl.ds(block * 4 + k, 1), :] for k in range(4)]
            high, low = split(jnp.concatenate(pairs, axis=0))
            for part in range(COLS // 256):
                cols = slice(part * 256, (part + 1) * 256)
                held = weight[:, cols]
                sums = (dot(high, held) + dot(low, held)) * inside[:, cols]
                for k in range(4):
                    ridge = jnp.where(eye_row[:, cols] == block * 4 + k, damping, 0.0)
                    gram[block * 4 + k, :, cols] = sums[k * MODES : (k + 1) * MODES] + ridge

    def factor():
        @pl.loop(0, MODES)
        def _(k):
            scale = lax.rsqrt(gram[k, pl.ds(k, 1), :])
            column = jnp.where(eye_row >= k, gram[k] * scale, 0.0)
            gram[k] = column

            @pl.loop(k + 1, MODES)
            def _(j):
                gram[j] = gram[j] - gram[k] * gram[k, pl.ds(j, 1), :]

    def project(turn, owner, out, own=False):
        cols = TURNS[turn]
        if not own:
            flags = got_mask.at[owner, :, :, slice(cols.start // 2, cols.stop // 2)]
            pltpu.make_async_copy(flags, flags, mask_sem.at[turn, owner]).wait()
        values = got_vis.at[owner, :, cols]
        pltpu.make_async_copy(values, values, vis_sem.at[turn, owner]).wait()

        @pl.loop(cols.start // (2 * LANES), cols.stop // (2 * LANES))
        def _(group):
            narrow = pl.ds(pl.multiple_of(group * LANES, LANES), LANES)
            wide = pl.ds(pl.multiple_of(group * 2 * LANES, 2 * LANES), 2 * LANES)
            flags = jnp.concatenate([got_mask[owner, yy, :, narrow] for yy in range(NY)], axis=0)
            kept = widen((1 - flags).astype(F32))
            high, low = split(kept * got_vis[owner, :, wide])
            out[:, wide] = dot(chosen[...], jnp.concatenate([high, low, high], axis=0))

    pieces = pl.ds(0, MODES // 2), pl.ds(MODES // 2, MODES // 2)
    sends = {}

    def send(turn, way, slot):
        piece = (way, slot, pieces[way] if slot == 0 else pl.ds(0, MODES), TURNS[turn])
        sends[turn, way, slot] = pltpu.make_async_remote_copy(
            src_ref=partial.at[piece],
            dst_ref=chain.at[piece],
            send_sem=chain_send.at[turn, way, slot],
            recv_sem=chain_sem.at[turn, way, slot],
            device_id={"chan": at(y, ahead(1 - 2 * way), core)},
            device_id_type=MESH,
        )
        sends[turn, way, slot].start()

    def begin(turn):
        cols = TURNS[turn]
        project(turn, ahead(4), partial.at[0, 0])
        partial[1, 0, MODES // 2 :, cols] = partial[0, 0, MODES // 2 :, cols]
        for way in range(2):
            send(turn, way, 0)

    def step_on(turn, slot):
        for way in range(2):
            project(turn, ahead((4 - slot) * (1 - 2 * way)), partial.at[way, slot])
            rows = pieces[way] if slot == 1 else pl.ds(0, MODES)
            cols = TURNS[turn]
            sends[turn, way, slot - 1].wait_recv()
            partial[way, slot, rows, cols] = partial[way, slot, rows, cols] + chain[way, slot - 1, rows, cols]
            send(turn, way, slot)

    def conclude(turn):
        cols = TURNS[turn]
        project(turn, z, answer, own=True)
        for way in range(2):
            sends[turn, way, 3].wait_recv()
        answer[:, cols] = (answer[:, cols] + chain[0, 3, :, cols] + chain[1, 3, :, cols]) * valid[:, cols]

        @pl.loop(0, MODES)
        def _(k):
            row = answer[pl.ds(k, 1), cols] / gram[k, pl.ds(k, 1), cols]
            answer[:, cols] = answer[:, cols] - jnp.where(eye_row[:, cols] > k, gram[k, :, cols] * row, 0.0)
            answer[pl.ds(k, 1), cols] = row

        coef = coefs.at[y, z, core]
        coef[:, cols] = jnp.zeros((MODES, cols.stop - cols.start), F32)

        @pl.loop(0, MODES)
        def _(step):
            k = MODES - 1 - step
            later = jnp.sum(gram[k, :, cols] * coef[:, cols], axis=0, keepdims=True)
            coef[pl.ds(k, 1), cols] = (answer[pl.ds(k, 1), cols] - later) / gram[k, pl.ds(k, 1), cols]


    def push(piece, peer, arrived, sent=None):
        pltpu.make_async_remote_copy(
            src_ref=piece,
            dst_ref=piece,
            send_sem=link_send.at[0] if sent is None else sent,
            recv_sem=arrived,
            device_id={"chan": peer},
            device_id_type=MESH,
        ).start()

    def wait(piece, arrived):
        pltpu.make_async_copy(piece, piece, arrived).wait()

    def beside(way):
        return at(y, ahead(1 - 2 * way), core)

    def finish(half, *places):
        cols = (FIRST, SECOND)[half]
        results = []
        for place in places:
            high, low = split(coefs[(*place, slice(None), cols)])
            model = dot(basis[...], jnp.concatenate([high, low, high], axis=0))
            results.append(kept_vis[at(*place), :, cols] - model)
        for place, result in zip(places, results):
            start = pl.multiple_of(at(*place) * COLS + cols.start, LANES)
            out[:, pl.ds(start, cols.stop - cols.start)] = result

    def hand(half, yy, zz):
        cols = (FIRST, SECOND)[half]
        push(coefs.at[yy, zz, core, :, cols], at(y, z, 1 - core), twin_sem.at[half, yy, zz], twin_send.at[0])

    def along(yy, zz, way, far):
        def go():
            push(coefs.at[yy, zz, core, :, FIRST], beside(way), along_sem.at[way, far, yy])

        if far < 4:
            go()
        elif far == 4:
            pl.when(yy % 2 == way)(go)

    def first(zz, way, far):
        if far < 4:
            push(coefs.at[y, zz, core, :, SECOND], beside(way), first_sem.at[way, far])
        elif far == 4:
            push(coefs.at[y, zz, core, :, SECOND_OF[way]], beside(way), first_sem.at[way, far])

    def above(way):
        return at((y + 1 - 2 * way + NY) % NY, z, core)

    def spread(zz):
        for way in range(2):
            push(coefs.at[y, zz, core, :, SECOND], above(way), spread_sem.at[way, zz])

    def start_second():
        pltpu.make_async_copy(kept_vis, kept_vis, load_sem.at[0]).wait()
        for way in range(2):
            first(z, way, 1)
        spread(z)
        hand(1, y, z)
        finish(1, (y, z, core))

    def start_first():
        for step in (1, 3, 2):
            push(coefs.at[y, z, core, :, FIRST], at((y + step) % NY, z, core), across_sem.at[y])
        for way in range(2):
            along(y, z, way, 1)
        hand(0, y, z)
        finish(0, (y, z, core))

    def origin(way, far):
        return ahead(far * (2 * way - 1))

    def second_of(far):
        if far == 4:
            zz = ahead(4)
            for way in range(2):
                wait(coefs.at[y, zz, core, :, SECOND_OF[way]], first_sem.at[way, 4])
            spread(zz)
            hand(1, y, zz)
            finish(1, (y, zz, core))
            return
        for way in range(2):
            zz = origin(way, far)
            wait(coefs.at[y, zz, core, :, SECOND], first_sem.at[way, far])
            first(zz, way, far + 1)
            spread(zz)
            hand(1, y, zz)
        finish(1, *[(y, origin(way, far), core) for way in range(2)])

    def near(far):
        return (z,) if far == 0 else (ahead(4),) if far == 4 else (ahead(far), ahead(-far))

    def second_spread(far):
        for zz in near(far):
            for way in range(2):
                yy = (y + 2 * way - 1 + NY) % NY
                wait(coefs.at[yy, zz, core, :, SECOND], spread_sem.at[way, zz])

                @pl.when(zz % 2 == way)
                def _():
                    push(coefs.at[yy, zz, core, :, SECOND], above(way), relay_sem.at[zz])

                hand(1, yy, zz)
        finish(1, *[((y + step) % NY, zz, core) for zz in near(far) for step in (1, 3)])

    def second_relay(far):
        yy = (y + 2) % NY
        for zz in near(far):
            wait(coefs.at[yy, zz, core, :, SECOND], relay_sem.at[zz])
            hand(1, yy, zz)
        finish(1, *[(yy, zz, core) for zz in near(far)])

    def first_across():
        @pl.loop(1, NY)
        def _(step):
            yy = (y + step) % NY
            wait(coefs.at[yy, z, core, :, FIRST], across_sem.at[yy])
            for way in range(2):
                along(yy, z, way, 1)
            hand(0, yy, z)

        finish(0, *[((y + step) % NY, z, core) for step in range(1, NY)])

    def first_of(far):
        @pl.loop(0, NY)
        def _(step):
            yy = (y + step) % NY
            if far == 4:
                zz = ahead(4)
                wait(coefs.at[yy, zz, core, :, FIRST], along_sem.at[yy % 2, 4, yy])
                hand(0, yy, zz)
                return
            for way in range(2):
                zz = origin(way, far)
                wait(coefs.at[yy, zz, core, :, FIRST], along_sem.at[way, far, yy])
                along(yy, zz, way, far + 1)
                hand(0, yy, zz)

        finish(0, *[(yy, zz, core) for yy in range(NY) for zz in near(far)])

    def taken(half, far):
        @pl.loop(0, NY)
        def _(yy):
            for zz in near(far):
                wait(coefs.at[yy, zz, 1 - core, :, (FIRST, SECOND)[half]], twin_sem.at[half, yy, zz])

        finish(half, *[(yy, zz, 1 - core) for yy in range(NY) for zz in near(far)])

    send_mask(0, 4, 3, -3)
    send_vis()
    weigh()
    make_gram()
    begin(0)
    send_mask(0, 2, -2)
    factor()
    step_on(0, 1)
    send_mask(0, 1, -1)
    send_mask(1, 4)
    step_on(0, 2)
    send_mask(1, 3, -3)
    begin(1)
    step_on(0, 3)
    send_mask(1, 2, -2)
    step_on(1, 1)
    send_mask(1, 1, -1)
    conclude(0)
    start_second()
    step_on(1, 2)
    second_of(1)
    step_on(1, 3)
    second_spread(0)
    second_of(2)
    conclude(1)
    start_first()
    second_spread(1)
    second_relay(0)
    first_across()
    second_of(3)
    taken(1, 0)
    first_of(1)
    second_spread(2)
    second_relay(1)
    second_of(4)
    first_of(2)
    taken(1, 1)
    second_spread(3)
    second_relay(2)
    first_of(3)
    taken(0, 0)
    taken(1, 2)
    second_spread(4)
    second_relay(3)
    first_of(4)
    taken(0, 1)
    taken(0, 2)
    second_relay(4)
    taken(1, 3)
    taken(0, 3)
    taken(0, 4)
    taken(1, 4)

    pltpu.make_async_copy(gram.at[: MODES - 1], gram.at[: MODES - 1], link_send.at[0]).wait()
    pltpu.make_async_copy(gram, gram, twin_send.at[0]).wait()
    for s in sends.values():
        s.wait_send()
    sent = flipped.at[:, pl.ds(0, (NX - 1) * SLAB)]
    pltpu.make_async_copy(sent, sent, send_sem.at[0]).wait()
    sent = got_mask.at[pl.ds(0, NZ - 1)]
    pltpu.make_async_copy(sent, sent, send_sem.at[1]).wait()
    sent = got_vis.at[pl.ds(0, NY * NC - 1)]
    pltpu.make_async_copy(sent, sent, send_sem.at[2]).wait()


def fit(vis, mask, modes, counts):
    outside = pl.BlockSpec(memory_space=pltpu.HBM)
    held = pl.BlockSpec(memory_space=pltpu.VMEM)
    return pl.pallas_call(
        fit_kernel,
        out_shape=jax.ShapeDtypeStruct(vis.shape, F32),
        in_specs=[outside, held, held, held],
        out_specs=held,
        scratch_shapes=[
            pltpu.VMEM((1, COLS), F32),
            pltpu.VMEM((NY, NZ, NC, MODES, COLS), F32),
            pltpu.VMEM((ROWS, 3 * MODES), BF16),
            pltpu.VMEM((NY * NZ * NC, ROWS, COLS), F32),
            pltpu.VMEM((NX * SLAB, LANES), F32),
            pltpu.VMEM((NZ, NY, NC * ROWS, HALF), jnp.int32),
            pltpu.VMEM((NZ, SEL, COLS), F32),
            pltpu.VMEM((NX * SLAB, COLS), BF16),
            pltpu.VMEM((MODES, MODES, COLS), F32),
            pltpu.VMEM((MODES, NX * SLAB), F32),
            pltpu.VMEM((MODES, 3 * SEL), BF16),
            pltpu.VMEM((2, 4, MODES, COLS), F32),
            pltpu.VMEM((2, 4, MODES, COLS), F32),
            pltpu.VMEM((MODES, COLS), F32),
            pltpu.SemaphoreType.DMA((1,)),
            pltpu.SemaphoreType.DMA((2, NZ)),
            pltpu.SemaphoreType.DMA((2, NZ)),
            pltpu.SemaphoreType.DMA((2, 2, 4)),
            pltpu.SemaphoreType.DMA((3,)),
            pltpu.SemaphoreType.DMA((2, 2, 4)),
            pltpu.SemaphoreType.DMA((NY,)),
            pltpu.SemaphoreType.DMA((2, 5, NY)),
            pltpu.SemaphoreType.DMA((2, 5)),
            pltpu.SemaphoreType.DMA((2, NZ)),
            pltpu.SemaphoreType.DMA((NZ,)),
            pltpu.SemaphoreType.DMA((2, NY, NZ)),
            pltpu.SemaphoreType.DMA((1,)),
            pltpu.SemaphoreType.DMA((1,)),
            pltpu.SemaphoreType.DMA((1,)),
        ],
        compiler_params=pltpu.CompilerParams(
            collective_id=0, has_side_effects=True, vmem_limit_bytes=44 * 1024 * 1024
        ),
        name="fit",
    )(vis, mask, modes, counts)


def per_device(visibility, interference_mask, valid_time_count, fit_modes):
    mask = interference_mask.reshape(NY, NZ, NC * ROWS, HALF)
    return fit(visibility, mask, fit_modes.T, valid_time_count.reshape(1, -1))


def solution(mesh):
    placed = (P("chan", "grp"), P(None, ("grp", "chan")), P(("grp", "chan")), P("grp", None))
    return jax.shard_map(
        per_device, mesh=mesh, in_specs=placed, out_specs=P("chan", "grp"), check_vma=False
    )
```

time: 115 us -> 105 us (0.913)
  Pallas kernels: 107 us -> 100 us
  local copies, waits for them, and re-layouts: 6.68 us -> 5.02 us
    pallas_call x1, Pallas kernels: 107 us -> 100 us  [fit(): pl.pallas_call(fit_kernel, out_shape=jax.ShapeDtypeStruct(vis.shape, F32)...]
    unnamed x2 -> x7, local copies, waits for them, and re-layouts: 5.32 us -> 5.02 us
where the time goes in v3:
time: 105 us
  Pallas kernels  100 us (95%)
  local copies, waits for them, and re-layouts  5.02 us (5%)
    pallas_call x1, Pallas kernels, fit(): pl.pallas_call(fit_kernel, out_shape=jax.ShapeDtypeStruct(vis.shape, F32)...  100 us
    unnamed x7, local copies, waits for them, and re-layouts  5.02 us

profile of v3, /device:TPU:1, one launch (start us, length us, event | category | flops | bytes accessed | tf_op | source)
XLA Modules:
  0.0 105.1 jit_solution(17606047877260797132)
XLA Ops:
  0.0 0.0 copy-start
  0.0 1.6 %copy-done = s32[1024,512]{1,0:T(8,128)S(1)} copy-done((s32[1024,512]{1,0:T(8,128)S(1)}, s32[1024,512]{1,0:T(8,128)}, u32[]{:S(2)}) %copy-start) | copy-done | bytes 2097176
  1.6 0.0 copy-start.1
  1.6 0.8 copy-done.1
  2.4 0.0 copy-start.2
  2.4 0.7 copy-done.2
  3.0 100.1 %fit.1 = f32[16,65536]{1,0:T(8,128)S(1)} custom-call(f32[16,65536]{1,0:T(8,128)} %vis.1, s32[4,8,32,512]{3,2,1,0:T(8,128)S(1)} %bitcast.3, f32[32,256]{1,0:T(8,128)S(1)} %bitcast.4, s32[1,16]{1,0:T(1,128)S(1)} %bitcast.5), custom_call_target="tpu_custom_call" | custom-call | tf_op jit(solution)/shard_map/fit/pallas_call | solution.py:515
  103.1 2.0 %copy.6 = f32[16,65536]{1,0:T(8,128)} copy(f32[16,65536]{1,0:T(8,128)S(1)} %fit.1) | data formatting | bytes 8388608
Async XLA Ops:
  0.0 1.6 %copy-start = (s32[1024,512]{1,0:T(8,128)S(1)}, s32[1024,512]{1,0:T(8,128)}, u32[]{:S(2)}) copy-start(s32[1024,512]{1,0:T(8,128)} %param.5) | copy-start | bytes 6291460
  1.6 0.8 copy-start.1
  2.4 0.7 copy-start.2

commit v4 on v3

--- a/solution.py
+++ b/solution.py
@@ -323,9 +323,9 @@
             start = pl.multiple_of(at(*place) * COLS + cols.start, LANES)
             out[:, pl.ds(start, cols.stop - cols.start)] = result
 
-    def hand(half, yy, zz):
+    def hand(half, yy, zz, far):
         cols = (FIRST, SECOND)[half]
-        push(coefs.at[yy, zz, core, :, cols], at(y, z, 1 - core), twin_sem.at[half, yy, zz], twin_send.at[0])
+        push(coefs.at[yy, zz, core, :, cols], at(y, z, 1 - core), twin_sem.at[half, far], twin_send.at[0])
 
     def along(yy, zz, way, far):
         def go():
@@ -354,7 +354,7 @@
         for way in range(2):
             first(z, way, 1)
         spread(z)
-        hand(1, y, z)
+        hand(1, y, z, 0)
         finish(1, (y, z, core))
 
     def start_first():
@@ -362,7 +362,7 @@
             push(coefs.at[y, z, core, :, FIRST], at((y + step) % NY, z, core), across_sem.at[y])
         for way in range(2):
             along(y, z, way, 1)
-        hand(0, y, z)
+        hand(0, y, z, 0)
         finish(0, (y, z, core))
 
     def origin(way, far):
@@ -374,7 +374,7 @@
             for way in range(2):
                 wait(coefs.at[y, zz, core, :, SECOND_OF[way]], first_sem.at[way, 4])
             spread(zz)
-            hand(1, y, zz)
+            hand(1, y, zz, far)
             finish(1, (y, zz, core))
             return
         for way in range(2):
@@ -382,30 +382,33 @@
             wait(coefs.at[y, zz, core, :, SECOND], first_sem.at[way, far])
             first(zz, way, far + 1)
             spread(zz)
-            hand(1, y, zz)
+            hand(1, y, zz, far)
         finish(1, *[(y, origin(way, far), core) for way in range(2)])
 
     def near(far):
         return (z,) if far == 0 else (ahead(4),) if far == 4 else (ahead(far), ahead(-far))
 
     def second_spread(far):
-        for zz in near(far):
+        for side, zz in enumerate(near(far)):
             for way in range(2):
                 yy = (y + 2 * way - 1 + NY) % NY
                 wait(coefs.at[yy, zz, core, :, SECOND], spread_sem.at[way, zz])
 
-                @pl.when(zz % 2 == way)
-                def _():
+                def relay():
                     push(coefs.at[yy, zz, core, :, SECOND], above(way), relay_sem.at[zz])
 
-                hand(1, yy, zz)
+                if far in (0, 4):
+                    pl.when(yy % 2 == way)(relay)
+                elif side == way:
+                    relay()
+                hand(1, yy, zz, far)
         finish(1, *[((y + step) % NY, zz, core) for zz in near(far) for step in (1, 3)])
 
     def second_relay(far):
         yy = (y + 2) % NY
         for zz in near(far):
             wait(coefs.at[yy, zz, core, :, SECOND], relay_sem.at[zz])
-            hand(1, yy, zz)
+            hand(1, yy, zz, far)
         finish(1, *[(yy, zz, core) for zz in near(far)])
 
     def first_across():
@@ -415,7 +418,7 @@
             wait(coefs.at[yy, z, core, :, FIRST], across_sem.at[yy])
             for way in range(2):
                 along(yy, z, way, 1)
-            hand(0, yy, z)
+            hand(0, yy, z, 0)
 
         finish(0, *[((y + step) % NY, z, core) for step in range(1, NY)])
 
@@ -426,22 +429,19 @@
             if far == 4:
                 zz = ahead(4)
                 wait(coefs.at[yy, zz, core, :, FIRST], along_sem.at[yy % 2, 4, yy])
-                hand(0, yy, zz)
+                hand(0, yy, zz, far)
                 return
             for way in range(2):
                 zz = origin(way, far)
                 wait(coefs.at[yy, zz, core, :, FIRST], along_sem.at[way, far, yy])
                 along(yy, zz, way, far + 1)
-                hand(0, yy, zz)
+                hand(0, yy, zz, far)
 
         finish(0, *[(yy, zz, core) for yy in range(NY) for zz in near(far)])
 
     def taken(half, far):
-        @pl.loop(0, NY)
-        def _(yy):
-            for zz in near(far):
-                wait(coefs.at[yy, zz, 1 - core, :, (FIRST, SECOND)[half]], twin_sem.at[half, yy, zz])
-
+        amount = coefs.at[:, : len(near(far)), 0, :, (FIRST, SECOND)[half]]
+        wait(amount, twin_sem.at[half, far])
         finish(half, *[(yy, zz, 1 - core) for yy in range(NY) for zz in near(far)])
 
     send_mask(0, 4, 3, -3)
@@ -467,33 +467,33 @@
     second_of(1)
     step_on(1, 3)
     second_spread(0)
-    second_of(2)
     conclude(1)
     start_first()
+    second_of(2)
     second_spread(1)
     second_relay(0)
     first_across()
     second_of(3)
-    taken(1, 0)
+    second_spread(2)
     first_of(1)
-    second_spread(2)
     second_relay(1)
     second_of(4)
     first_of(2)
-    taken(1, 1)
     second_spread(3)
     second_relay(2)
     first_of(3)
+    taken(1, 0)
+    second_spread(4)
+    taken(1, 1)
+    first_of(4)
     taken(0, 0)
+    taken(0, 1)
+    second_relay(3)
     taken(1, 2)
-    second_spread(4)
-    second_relay(3)
-    first_of(4)
-    taken(0, 1)
     taken(0, 2)
     second_relay(4)
+    taken(0, 3)
     taken(1, 3)
-    taken(0, 3)
     taken(0, 4)
     taken(1, 4)
 
@@ -543,7 +543,7 @@
             pltpu.SemaphoreType.DMA((2, 5)),
             pltpu.SemaphoreType.DMA((2, NZ)),
             pltpu.SemaphoreType.DMA((NZ,)),
-            pltpu.SemaphoreType.DMA((2, NY, NZ)),
+            pltpu.SemaphoreType.DMA((2, 5)),
             pltpu.SemaphoreType.DMA((1,)),
             pltpu.SemaphoreType.DMA((1,)),
             pltpu.SemaphoreType.DMA((1,)),

time: 105 us -> 104 us (level)
  Pallas kernels: 100 us -> 98.5 us
    pallas_call x1, Pallas kernels: 100 us -> 98.5 us  [fit(): pl.pallas_call(fit_kernel, out_shape=jax.ShapeDtypeStruct(vis.shape, F32)...]
where the time goes in v4:
time: 104 us; the launch traced here: 103 us
  Pallas kernels  98.5 us (95%)
  local copies, waits for them, and re-layouts  5.02 us (5%)
    pallas_call x1, Pallas kernels, fit(): pl.pallas_call(fit_kernel, out_shape=jax.ShapeDtypeStruct(vis.shape, F32)...  98.5 us
    unnamed x7, local copies, waits for them, and re-layouts  5.02 us

profile of v4, /device:TPU:1, one launch (start us, length us, event | category | flops | bytes accessed | tf_op | source)
XLA Modules:
  0.0 103.5 jit_solution(4387216188862119057)
XLA Ops:
  0.0 0.0 copy-start
  0.0 1.6 %copy-done = s32[1024,512]{1,0:T(8,128)S(1)} copy-done((s32[1024,512]{1,0:T(8,128)S(1)}, s32[1024,512]{1,0:T(8,128)}, u32[]{:S(2)}) %copy-start) | copy-done | bytes 2097176
  1.6 0.0 copy-start.1
  1.6 0.8 copy-done.1
  2.4 0.0 copy-start.2
  2.4 0.7 copy-done.2
  3.0 98.5 %fit.1 = f32[16,65536]{1,0:T(8,128)S(1)} custom-call(f32[16,65536]{1,0:T(8,128)} %vis.1, s32[4,8,32,512]{3,2,1,0:T(8,128)S(1)} %bitcast.3, f32[32,256]{1,0:T(8,128)S(1)} %bitcast.4, s32[1,16]{1,0:T(1,128)S(1)} %bitcast.5), custom_call_target="tpu_custom_call" | custom-call | tf_op jit(solution)/shard_map/fit/pallas_call | solution.py:515
  101.5 2.0 %copy.6 = f32[16,65536]{1,0:T(8,128)} copy(f32[16,65536]{1,0:T(8,128)S(1)} %fit.1) | data formatting | bytes 8388608
Async XLA Ops:
  0.0 1.6 %copy-start = (s32[1024,512]{1,0:T(8,128)S(1)}, s32[1024,512]{1,0:T(8,128)}, u32[]{:S(2)}) copy-start(s32[1024,512]{1,0:T(8,128)} %param.5) | copy-start | bytes 6291460
  1.6 0.8 copy-start.1
  2.4 0.7 copy-start.2

commit v5 on v4

--- a/solution.py
+++ b/solution.py
@@ -55,6 +55,7 @@
     modes,
     counts,
     out,
+    inverse,
     valid,
     coefs,
     basis,
@@ -218,6 +219,7 @@
         @pl.loop(0, MODES)
         def _(k):
             scale = lax.rsqrt(gram[k, pl.ds(k, 1), :])
+            inverse[pl.ds(k, 1), :] = scale
             column = jnp.where(eye_row >= k, gram[k] * scale, 0.0)
             gram[k] = column
 
@@ -282,7 +284,7 @@
 
         @pl.loop(0, MODES)
         def _(k):
-            row = answer[pl.ds(k, 1), cols] / gram[k, pl.ds(k, 1), cols]
+            row = answer[pl.ds(k, 1), cols] * inverse[pl.ds(k, 1), cols]
             answer[:, cols] = answer[:, cols] - jnp.where(eye_row[:, cols] > k, gram[k, :, cols] * row, 0.0)
             answer[pl.ds(k, 1), cols] = row
 
@@ -293,7 +295,7 @@
         def _(step):
             k = MODES - 1 - step
             later = jnp.sum(gram[k, :, cols] * coef[:, cols], axis=0, keepdims=True)
-            coef[pl.ds(k, 1), cols] = (answer[pl.ds(k, 1), cols] - later) / gram[k, pl.ds(k, 1), cols]
+            coef[pl.ds(k, 1), cols] = (answer[pl.ds(k, 1), cols] - later) * inverse[pl.ds(k, 1), cols]
 
 
     def push(piece, peer, arrived, sent=None):
@@ -474,14 +476,14 @@
     second_relay(0)
     first_across()
     second_of(3)
+    first_of(1)
     second_spread(2)
-    first_of(1)
     second_relay(1)
     second_of(4)
     first_of(2)
     second_spread(3)
+    first_of(3)
     second_relay(2)
-    first_of(3)
     taken(1, 0)
     second_spread(4)
     taken(1, 1)
@@ -518,6 +520,7 @@
         in_specs=[outside, held, held, held],
         out_specs=held,
         scratch_shapes=[
+            pltpu.VMEM((MODES, COLS), F32),
             pltpu.VMEM((1, COLS), F32),
             pltpu.VMEM((NY, NZ, NC, MODES, COLS), F32),
             pltpu.VMEM((ROWS, 3 * MODES), BF16),

time: 104 us -> 104 us (level)
  no operation moved by 1% of the time
where the time goes in v5:
time: 104 us; the launch traced here: 103 us
  Pallas kernels  98.3 us (95%)
  local copies, waits for them, and re-layouts  5.02 us (5%)
    pallas_call x1, Pallas kernels, fit(): pl.pallas_call(fit_kernel, out_shape=jax.ShapeDtypeStruct(vis.shape, F32)...  98.3 us
    unnamed x7, local copies, waits for them, and re-layouts  5.02 us

profile of v5, /device:TPU:1, one launch (start us, length us, event | category | flops | bytes accessed | tf_op | source)
XLA Modules:
  0.0 103.3 jit_solution(11531288821588425188)
XLA Ops:
  0.0 0.0 copy-start
  0.0 1.6 %copy-done = s32[1024,512]{1,0:T(8,128)S(1)} copy-done((s32[1024,512]{1,0:T(8,128)S(1)}, s32[1024,512]{1,0:T(8,128)}, u32[]{:S(2)}) %copy-start) | copy-done | bytes 2097176
  1.6 0.0 copy-start.1
  1.6 0.8 copy-done.1
  2.4 0.0 copy-start.2
  2.4 0.7 copy-done.2
  3.0 98.3 %fit.1 = f32[16,65536]{1,0:T(8,128)S(1)} custom-call(f32[16,65536]{1,0:T(8,128)} %vis.1, s32[4,8,32,512]{3,2,1,0:T(8,128)S(1)} %bitcast.3, f32[32,256]{1,0:T(8,128)S(1)} %bitcast.4, s32[1,16]{1,0:T(1,128)S(1)} %bitcast.5), custom_call_target="tpu_custom_call" | custom-call | tf_op jit(solution)/shard_map/fit/pallas_call | solution.py:517
  101.3 2.0 %copy.6 = f32[16,65536]{1,0:T(8,128)} copy(f32[16,65536]{1,0:T(8,128)S(1)} %fit.1) | data formatting | bytes 8388608
Async XLA Ops:
  0.0 1.6 %copy-start = (s32[1024,512]{1,0:T(8,128)S(1)}, s32[1024,512]{1,0:T(8,128)}, u32[]{:S(2)}) copy-start(s32[1024,512]{1,0:T(8,128)} %param.5) | copy-start | bytes 6291460
  1.6 0.8 copy-start.1
  2.4 0.7 copy-start.2
